TPU v7x, 128 devices: a whole 4x4x4 slice. The times are simulated.
128 devices in a mesh: seq: 32 (over x, y, core), head: 4 (over z).
Axes of the slice: x: 4, y: 4, z: 4, core: 2. Of those that a mesh axis runs over, the one named last changes fastest.
Arguments:
- queries: bfloat16 [8192, 4096], P('seq', 'head'), may hold values from -7.1875 to 7.1875
- keys: bfloat16 [8192, 1024], P(('seq', 'head')), may hold values from -7.1875 to 7.1875
- values: bfloat16 [8192, 1024], P(('seq', 'head')), may hold values from -6 to 6
- outputs: bfloat16 [8192, 4096], P('seq', 'head'), may hold values from -1.1953125 to 1.1953125
- out_grad: bfloat16 [8192, 4096], P('seq', 'head'), may hold values from -6 to 6
- log_norm: float32 [32, 8192], P('head', 'seq'), as said below
- block_order: int32 [64], replicated, may hold values from 0 to 63, as said below
Outputs:
- query_grad: bfloat16 [8192, 4096], P('seq', 'head')
- key_gradient_rows: bfloat16 [8192, 1024], P(('seq', 'head'))
- value_gradient_rows: bfloat16 [8192, 1024], P(('seq', 'head'))
Inputs may be any that keep to these rules, and one draw needn't show every extreme that they name: `block_order`: A permutation of 0 to 63. log_norm[h, i] lies within 0.6 of one plus the natural logarithm of 1 + pos[i].
All inputs are finite; a program needn't handle non-finite values.
Results may differ from a plain program's by a relative error of at most 0.014.
Values may be sent and summed in bfloat16 or wider, within the bound.
A program may use at most 192 MiB of HBM per device.

v0:
```python
import jax
import jax.numpy as jnp
from jax import lax
from jax.sharding import PartitionSpec as P

QUERY_HEADS = 32
KEY_VALUE_HEADS = 8
HEAD_SIZE = 128


def side_by_side(arrays, axis, dim, along):
    ends, at = ([], 0)
    for a in arrays[:-1]:
        at += a.shape[along]
        ends.append(at)
    both = jnp.concatenate(arrays, axis=along)
    return tuple(jnp.split(lax.all_gather(both, axis, axis=dim, tiled=True), ends, axis=along))


def row_positions(block_order, first_row, count, half):
    rows_here = first_row + jnp.arange(count, dtype=jnp.int32)
    blocks = rows_here // half
    table = jnp.arange(block_order.shape[0], dtype=jnp.int32)
    picked = jnp.sum(jnp.where(blocks[:, None] == table[None, :], block_order[None, :], 0), 1)
    return picked * half + rows_here % half


def masked_terms(q_blk, dout_blk, lse_blk, delta_blk, q_pos, k_blk, v_blk, k_pos):
    scale = HEAD_SIZE ** (-0.5)
    scores = jnp.einsum("tgrd,ngd->grtn", q_blk, k_blk, preferred_element_type=jnp.float32) * scale
    visible = k_pos[None, :] <= q_pos[:, None]
    prob = jnp.where(visible, jnp.exp(scores - lse_blk[..., None]), 0.0)
    dprob = jnp.einsum("tgrd,ngd->grtn", dout_blk, v_blk, preferred_element_type=jnp.float32)
    dscore = prob * (dprob - delta_blk[..., None])
    prob_low = prob.astype(jnp.bfloat16)
    dscore_low = dscore.astype(jnp.bfloat16)
    queries_gradient = (
        jnp.einsum("grtn,ngd->tgrd", dscore_low, k_blk, preferred_element_type=jnp.float32) * scale
    )
    keys_gradient = (
        jnp.einsum("grtn,tgrd->ngd", dscore_low, q_blk, preferred_element_type=jnp.float32) * scale
    )
    values_gradient = jnp.einsum(
        "grtn,tgrd->ngd", prob_low, dout_blk, preferred_element_type=jnp.float32
    )
    return (queries_gradient, keys_gradient, values_gradient)


def step_rows(count):
    step = count
    while step > 1024 and step % 2 == 0:
        step = step // 2
    return step


def local(queries, keys, values, outputs, out_grad, log_norm, block_order):
    index = lax.axis_index("seq")
    rows = queries.shape[0]
    half = rows // 2
    group_ratio = QUERY_HEADS // KEY_VALUE_HEADS
    k_loc, v_loc = (
        lax.all_to_all(keys, "head", split_axis=1, concat_axis=0, tiled=True),
        lax.all_to_all(values, "head", split_axis=1, concat_axis=0, tiled=True),
    )
    q_cols = queries.shape[1]
    heads_here = q_cols // HEAD_SIZE
    groups = heads_here // group_ratio
    k_cols = k_loc.shape[1]
    delta = jnp.sum(
        (out_grad.astype(jnp.float32) * outputs.astype(jnp.float32)).reshape(
            rows, heads_here, HEAD_SIZE
        ),
        -1,
    )
    own_pair = lax.dynamic_slice(block_order, (2 * index,), (2,))
    own_blocks = (own_pair[0], own_pair[1])
    offset = jnp.arange(half, dtype=jnp.int32)
    own_pos = jnp.concatenate([own_blocks[0] * half + offset, own_blocks[1] * half + offset], 0)
    k_own = k_loc.reshape(rows, groups, HEAD_SIZE)
    v_own = v_loc.reshape(rows, groups, HEAD_SIZE)
    keys_gradient = None
    values_gradient = None
    all_lse, all_delta = side_by_side((log_norm.T, delta), "seq", 0, 1)
    k_zero = jnp.zeros((rows, groups, HEAD_SIZE), jnp.float32)
    grad_k = k_zero
    grad_v = k_zero
    q_piece, dout_piece = side_by_side((queries, out_grad), "seq", 0, 1)
    count = q_piece.shape[0]
    step = step_rows(count)

    def one(acc, i):
        q_blk = lax.dynamic_slice_in_dim(q_piece, i * step, step, 0).reshape(
            step, groups, group_ratio, HEAD_SIZE
        )
        dout_blk = lax.dynamic_slice_in_dim(dout_piece, i * step, step, 0).reshape(
            step, groups, group_ratio, HEAD_SIZE
        )
        row0 = i * step
        lse_blk = lax.dynamic_slice_in_dim(all_lse, row0, step, 0).T.reshape(
            groups, group_ratio, step
        )
        delta_blk = lax.dynamic_slice_in_dim(all_delta, row0, step, 0).T.reshape(
            groups, group_ratio, step
        )
        q_pos = row_positions(block_order, row0, step, half)
        terms = masked_terms(q_blk, dout_blk, lse_blk, delta_blk, q_pos, k_own, v_own, own_pos)
        return ((acc[0] + terms[1], acc[1] + terms[2]), terms[0].reshape(step, q_cols))

    (grad_k, grad_v), stacked = lax.scan(
        one, (grad_k, grad_v), jnp.arange(count // step, dtype=jnp.int32)
    )
    grad_q_all = stacked.reshape(count, q_cols)
    grad_k, grad_v, grad_q_all = (grad_k, grad_v, grad_q_all)
    queries_gradient = lax.psum_scatter(
        grad_q_all.astype(jnp.bfloat16), "seq", scatter_dimension=0, tiled=True
    )
    keys_gradient = grad_k.reshape(rows, k_cols)
    values_gradient = grad_v.reshape(rows, k_cols)
    low_k = keys_gradient.astype(jnp.bfloat16)
    low_v = values_gradient.astype(jnp.bfloat16)
    key_gradient_rows, value_gradient_rows = (
        lax.all_to_all(low_k, "head", split_axis=0, concat_axis=1, tiled=True),
        lax.all_to_all(low_v, "head", split_axis=0, concat_axis=1, tiled=True),
    )
    return (queries_gradient, key_gradient_rows, value_gradient_rows)


def solution(mesh):
    in_specs = (
        P("seq", "head"),
        P(("seq", "head"), None),
        P(("seq", "head"), None),
        P("seq", "head"),
        P("seq", "head"),
        P("head", "seq"),
        P(),
    )
    out_specs = (P("seq", "head"), P(("seq", "head"), None), P(("seq", "head"), None))
    return jax.shard_map(local, mesh=mesh, in_specs=in_specs, out_specs=out_specs, check_vma=False)
```

profile of v0, /device:TPU:1, one launch (start us, length us, event | category | flops | bytes accessed | tf_op | source)
XLA Modules:
  0.0 431.3 jit_solution(8957605507295440083)
XLA Ops:
  10.8 1.6 copy.107
  12.4 5.8 %all-to-all-start = ((bf16[64,4,256]{2,0,1:T(8,128)(2,1)}), bf16[64,4,256]{2,0,1:T(8,128)(2,1)S(1)}, u32[]{:S(2)}, u32[]{:S(2)}) async-start(bf16[64,4,256]{2,0,1:T(8,128)(2,1)} %bitcast.94), calls=%async_computation | async-start | bytes 262144 | tf_op jit(solution)/shard_map/all_to_all | solution.py:62
  20.8 1.6 copy.106
  22.4 1.4 multiply_bitcast_fusion
  24.4 26.7 %all_gather.7 = f32[8192,16]{0,1:T(8,128)S(1)} all-gather(f32[256,16]{0,1:T(8,128)S(1)} %pad_maximum_fusion.1), channel_id=1, replica_groups=mesh['seq'=32,'head'=4] {'seq'}, dimensions={0}, use_global_device_ids=true | all-gather | bytes 540672 | tf_op jit(solution)/shard_map/all_gather | solution.py:17
  51.2 4.5 %all-to-all-start.1 = ((bf16[64,4,256]{2,0,1:T(8,128)(2,1)}), bf16[64,4,256]{2,0,1:T(8,128)(2,1)S(1)}, u32[]{:S(2)}, u32[]{:S(2)}) async-start(bf16[64,4,256]{2,0,1:T(8,128)(2,1)} %bitcast.93), calls=%async_computation.1 | async-start | bytes 262144 | tf_op jit(solution)/shard_map/all_to_all | solution.py:63
  55.9 4.7 %all-to-all-done.1 = bf16[64,4,256]{2,0,1:T(8,128)(2,1)S(1)} async-done(((bf16[64,4,256]{2,0,1:T(8,128)(2,1)}), bf16[64,4,256]{2,0,1:T(8,128)(2,1)S(1)}, u32[]{:S(2)}, u32[]{:S(2)}) %all-to-all-start.1) | async-done | bytes 131104 | tf_op jit(solution)/shard_map/all_to_all | solution.py:63
  60.6 79.5 %all-gather.2.cloned.1.call-done = bf16[8192,2048]{0,1:T(8,128)(2,1)} async-done(((bf16[256,2048]{0,1:T(8,128)(2,1)}), bf16[8192,2048]{0,1:T(8,128)(2,1)}) %all-gather.2.cloned.1.call-update) | async-done | bytes 33554448 | tf_op jit(solution)/shard_map/all_gather | solution.py:17
  140.1 22.9 %fusion.29 = (bf16[8192,1024]{0,1:T(8,128)(2,1)}, bf16[8192,1024]{0,1:T(8,128)(2,1)}) fusion(bf16[8192,2048]{0,1:T(8,128)(2,1)} %all-gather.2.cloned.1.call-done), kind=kLoop, calls=%fused_computation.51 | loop fusion | bytes 67108864 | tf_op jit(solution)/shard_map/split | solution.py:17
  163.1 125.2 %while.17 = (s32[]{:T(128)}, f32[256,2,128]{0,2,1:T(8,128)S(1)}, f32[256,2,128]{0,2,1:T(8,128)S(1)}, bf16[8,1024,1024]{1,2,0:T(8,128)(2,1)}, s32[8]{0:T(128)S(1)...) while((s32[]{:T(128)}, f32[256,2,128]{0,2,1:T(8,128)S(1)}, ...), condition=%wide.region_3.4_spmd.clone, body=%wide.region_1.3_spmd.clone.sunk | while | flops 2708239360 | bytes 63432188 | solution.py:109
  164.7 2.7 constant_dynamic-slice_fusion.3
  167.4 1.3 fusion.63
  168.7 2.0 fusion.67
  170.7 4.2 fusion.65
  175.7 1.5 convolution_multiply_fusion.2
  177.2 1.5 constant_dynamic-update-slice_fusion.2
  180.4 2.7 constant_dynamic-slice_fusion.3
  183.1 1.3 fusion.63
  184.4 2.0 fusion.67
  186.3 4.2 fusion.65
  191.3 1.5 convolution_multiply_fusion.2
  192.9 1.6 constant_dynamic-update-slice_fusion.2
  196.1 2.7 constant_dynamic-slice_fusion.3
  198.8 1.3 fusion.63
  200.1 2.0 fusion.67
  202.0 4.2 fusion.65
  207.0 1.5 convolution_multiply_fusion.2
  208.6 1.5 constant_dynamic-update-slice_fusion.2
  211.7 2.7 constant_dynamic-slice_fusion.3
  214.4 1.3 fusion.63
  215.7 2.0 fusion.67
  217.7 4.2 fusion.65
  222.7 1.5 convolution_multiply_fusion.2
  224.2 1.5 constant_dynamic-update-slice_fusion.2
  227.3 2.7 constant_dynamic-slice_fusion.3
  230.0 1.3 fusion.63
  231.3 2.0 fusion.67
  233.3 4.2 fusion.65
  238.3 1.5 convolution_multiply_fusion.2
  239.8 1.6 constant_dynamic-update-slice_fusion.2
  243.0 2.7 constant_dynamic-slice_fusion.3
  245.7 1.3 fusion.63
  247.0 2.0 fusion.67
  249.0 4.2 fusion.65
  254.0 1.5 convolution_multiply_fusion.2
  255.5 1.5 constant_dynamic-update-slice_fusion.2
  258.7 2.7 constant_dynamic-slice_fusion.3
  261.3 1.3 fusion.63
  262.6 2.0 fusion.67
  264.6 4.2 fusion.65
  269.6 1.5 convolution_multiply_fusion.2
  271.1 1.5 constant_dynamic-update-slice_fusion.2
  274.3 2.7 constant_dynamic-slice_fusion.3
  277.0 1.3 fusion.63
  278.3 2.0 fusion.67
  280.3 4.2 fusion.65
  285.3 1.5 convolution_multiply_fusion.2
  286.8 1.5 constant_dynamic-update-slice_fusion.2
  288.3 21.6 %copy.85 = bf16[8,1024,1024]{2,1,0:T(8,128)(2,1)} copy(bf16[8,1024,1024]{1,2,0:T(8,128)(2,1)} %get-tuple-element.169) | data formatting | bytes 33554432 | tf_op jit(solution)/shard_map/convert_element_type | solution.py:115
  310.8 4.1 all-to-all-start.2
  315.8 3.9 all-to-all-done.2
  319.7 3.3 all-to-all-start.3
  323.7 4.1 all-to-all-done.3
  328.5 95.9 %reduce-scatter.2.cloned.1.call-done = bf16[256,1024]{1,0:T(8,128)(2,1)} async-done(((bf16[8192,1024]{1,0:T(8,128)(2,1)}), bf16[256,1024]{1,0:T(8,128)(2,1)}) %reduce-scatter.2.cloned.1.call-update) | async-done | bytes 524304 | tf_op jit(solution)/shard_map/reduce_scatter | solution.py:114
  (109 shorter events, 22.6 us)
Async XLA Ops:
  7.2 17.3 %copy-start.1 = (f32[8,256]{1,0:T(8,128)S(1)}, f32[8,256]{1,0:T(8,128)}, u32[]{:S(2)}) copy-start(f32[8,256]{1,0:T(8,128)} %param.14) | copy-start | bytes 24580
  7.2 132.9 %all-gather.2.cloned.1.call-start = ((), (), s32[]{:S(2)}) async-start(), calls=%async_computation.5 | async-start | bytes 34603008 | tf_op jit(solution)/shard_map/all_gather | solution.py:17
  12.4 38.9 %all-to-all-start = ((bf16[64,4,256]{2,0,1:T(8,128)(2,1)}), bf16[64,4,256]{2,0,1:T(8,128)(2,1)S(1)}, u32[]{:S(2)}, u32[]{:S(2)}) async-start(bf16[64,4,256]{2,0,1:T(8,128)(2,1)} %bitcast.94), calls=%async_computation | async-start | bytes 262144 | tf_op jit(solution)/shard_map/all_to_all | solution.py:62
  51.2 9.3 %all-to-all-start.1 = ((bf16[64,4,256]{2,0,1:T(8,128)(2,1)}), bf16[64,4,256]{2,0,1:T(8,128)(2,1)S(1)}, u32[]{:S(2)}, u32[]{:S(2)}) async-start(bf16[64,4,256]{2,0,1:T(8,128)(2,1)} %bitcast.93), calls=%async_computation.1 | async-start | bytes 262144 | tf_op jit(solution)/shard_map/all_to_all | solution.py:63
  55.7 368.7 %reduce-scatter.2.cloned.1.call-start = ((), (), s32[]{:S(2)}) async-start(), calls=%async_computation.6 | async-start | bytes 17301504 | tf_op jit(solution)/shard_map/reduce_scatter | solution.py:114
  60.6 102.4 %copy-start = (s32[64]{0:T(128)S(1)}, s32[64]{0:T(128)}, u32[]{:S(2)}) copy-start(s32[64]{0:T(128)} %param.15) | copy-start | bytes 772
  310.8 9.0 %all-to-all-start.2 = ((bf16[4,64,256]{2,1,0:T(8,128)(2,1)}), bf16[4,64,256]{2,1,0:T(8,128)(2,1)S(1)}, u32[]{:S(2)}, u32[]{:S(2)}) async-start(bf16[4,64,256]{2,1,0:T(8,128)(2,1)} %convert_element_type.43), calls=%async_computation.3 | async-start | bytes 262144 | tf_op jit(solution)/shard_map/all_to_all | solution.py:122
  319.7 8.1 %all-to-all-start.3 = ((bf16[4,64,256]{2,1,0:T(8,128)(2,1)}), bf16[4,64,256]{2,1,0:T(8,128)(2,1)S(1)}, u32[]{:S(2)}, u32[]{:S(2)}) async-start(bf16[4,64,256]{2,1,0:T(8,128)(2,1)} %convert_element_type.45), calls=%async_computation.4 | async-start | bytes 262144 | tf_op jit(solution)/shard_map/all_to_all | solution.py:123
Sparse Core Ops, SparseCore 0:
  10.9 129.1 all-gather.1
  310.0 114.3 reduce-scatter.1
where the time goes:
time: 433 us; the launch traced here: 431 us
  waiting for transfers between devices  188 us (43%)
  local copies, waits for them, and re-layouts  93.6 us (22%)
  matrix products  78.1 us (18%)
  blocking collectives  26.7 us (6%)
  starting transfers between devices  17.8 us (4%)
  between operations  15.4 us (4%)
  loops' own time  5.91 us (1%)
  other arithmetic  5.56 us (1%)
    reduce_scatter x1, waiting for transfers between devices, local(): lax.psum_scatter(grad_q_all.astype(jnp.bfloat16), 'seq', scatter_dimensio...  95.9 us
    all_gather x1, waiting for transfers between devices, side_by_side(): lax.all_gather(both, axis, axis=dim, tiled=True)  79.5 us
    dot_general x8, matrix products, masked_terms(): jnp.einsum('tgrd,ngd->grtn', dout_blk, v_blk, preferred_element_type=jnp....  33.9 us
    all_gather x1, blocking collectives, side_by_side(): lax.all_gather(both, axis, axis=dim, tiled=True)  26.7 us
    split x2, local copies, waits for them, and re-layouts, side_by_side(): jnp.split(lax.all_gather(both, axis, axis=dim, tiled=True), ends, axis=al...  23 us
    convert_element_type x1, local copies, waits for them, and re-layouts, local(): grad_q_all.astype(jnp.bfloat16)  21.6 us
    dynamic_slice x8, local copies, waits for them, and re-layouts, one(): lax.dynamic_slice_in_dim(dout_piece, i * step, step, 0)  21.4 us
    dot_general x8, matrix products, masked_terms(): jnp.einsum('grtn,tgrd->ngd', prob_low, dout_blk, preferred_element_type=j...  15.7 us
  transfers between devices with their start and end apart: 6, of which 5 were waited for; matrix products, arithmetic and copies ran while one was open for 2% of the time, Pallas kernels for 0%

commit v1 on v0

v1 whole, which is shorter than its diff:
```python
import functools

import jax
import jax.numpy as jnp
from jax import lax
from jax.experimental import pallas as pl
from jax.experimental.pallas import tpu as pltpu
from jax.sharding import PartitionSpec as P

HEAD_SIZE = 128
RATIO = 4
SCALE = HEAD_SIZE ** (-0.5)
LOG2E = 1.4426950408889634
BIG = 131072.0
MESH = pl.DeviceIdType.MESH
BF = jnp.bfloat16
F32 = jnp.float32


def ring_order(i):
    return i + (i // 2) * (1 - 2 * (i % 2))


def chunk_of(t):
    j = t - 4
    near = jnp.where(t < 4, ring_order(t), ring_order(jnp.where(t < 12, j // 2, t - 12)))
    e = jnp.where(t < 4, 0, jnp.where(t < 12, 1 + 2 * (j % 2), 2))
    return near, e


def kernel(
    nz,
    q_ref, k_ref, v_ref, o_ref, do_ref, lse_ref, ktab_ref, qtab_ref,
    dq_ref, dk_ref, dv_ref,
    kv, sq, sdo, so, slse, qa, doa, qt, dot_, ktail, pbig, dsbig, dqacc,
    pbuf, r1, s2, r2, fin, dqs,
    s0s, s0r, sbs, sbr, axs, axr, ays, ayr, rks, rkr, rvs, rvr,
    r1s, r1r, r2s, r2r, s4s, s4r, dqss, dqsr,
):
    s = lax.axis_index("seq")
    z = lax.axis_index("head")
    x, y, c = s // 8, (s // 2) % 4, s % 2
    rows = q_ref.shape[0]
    piece = k_ref.shape[0]
    chip = 2 * rows
    blk = rows // 2
    half = RATIO * HEAD_SIZE
    nm = 2 * nz

    def dev(xx, yy, cc):
        return ((xx % 4) * 4 + (yy % 4)) * 2 + cc

    me = c * nz + z

    def member(r):
        m = (me + r) % nm
        return m // nz, m % nz

    barrier = pltpu.get_barrier_semaphore()
    for r in range(1, nm):
        cc, zz = member(r)
        pl.semaphore_signal(barrier, inc=1, device_id=(dev(x, y, cc), zz), device_id_type=MESH)
    for d in (1, 2, 3):
        pl.semaphore_signal(barrier, inc=1, device_id=(dev(x + d, y, c), z), device_id_type=MESH)
        pl.semaphore_signal(barrier, inc=1, device_id=(dev(x, y + d, c), z), device_id_type=MESH)
    pl.semaphore_wait(barrier, nm - 1 + 6)

    def rcopy(src, dst, ss, rs, to):
        return pltpu.make_async_remote_copy(
            src_ref=src, dst_ref=dst, send_sem=ss, recv_sem=rs,
            device_id=to, device_id_type=MESH)

    def s0_copy(r, w):
        cc, zz = member(r)
        g = pl.multiple_of((2 * zz + cc) * HEAD_SIZE, HEAD_SIZE)
        src = (k_ref, v_ref)[w].at[:, pl.ds(g, HEAD_SIZE)]
        off = pl.multiple_of(c * rows + z * piece, piece)
        return rcopy(src, kv.at[x, y, w, pl.ds(off, piece), :],
                     s0s.at[r, w], s0r.at[r, w], (dev(x, y, cc), zz))

    for r in range(1, nm):
        for w in range(2):
            s0_copy(r, w).start()

    other = pl.multiple_of((1 - c) * half, half)
    mine = pl.multiple_of(c * half, half)
    sib = (dev(x, y, 1 - c), z)
    sib_copies = [
        rcopy(q_ref.at[:, pl.ds(other, half)], sq, sbs.at[0], sbr.at[0], sib),
        rcopy(do_ref.at[:, pl.ds(other, half)], sdo, sbs.at[1], sbr.at[1], sib),
        rcopy(o_ref.at[:, pl.ds(other, half)], so, sbs.at[2], sbr.at[2], sib),
        rcopy(lse_ref, slse, sbs.at[3], sbr.at[3], sib),
    ]
    for cp in sib_copies:
        cp.start()

    own_off = pl.multiple_of(c * rows + z * piece, piece)
    own_g = pl.multiple_of((2 * z + c) * HEAD_SIZE, HEAD_SIZE)
    kv[x, y, 0, pl.ds(own_off, piece), :] = k_ref[:, pl.ds(own_g, HEAD_SIZE)]
    kv[x, y, 1, pl.ds(own_off, piece), :] = v_ref[:, pl.ds(own_g, HEAD_SIZE)]

    lane = lax.broadcasted_iota(jnp.int32, (blk, HEAD_SIZE), 1)

    def three(col, rest):
        hi = col.astype(BF).astype(F32)
        mid = (col - hi).astype(BF).astype(F32)
        lo = col - hi - mid
        return jnp.where(lane == 0, hi, jnp.where(lane == 1, mid, jnp.where(lane == 2, lo, rest))).astype(BF)

    chip_block = (x * 4 + y) * 4

    def prepare(qr, dor, orf, lr, col0, core):
        for b in range(2):
            rs = pl.ds(b * blk, blk)
            dst = pl.ds(pl.multiple_of(core * rows + b * blk, blk), blk)
            therm = jnp.broadcast_to(qtab_ref[pl.ds(chip_block + 2 * core + b, 1), :], (blk, HEAD_SIZE))
            zero = jnp.zeros((blk, HEAD_SIZE), F32)
            for h in range(RATIO):
                cols = pl.ds(pl.multiple_of(col0 + h * HEAD_SIZE, HEAD_SIZE), HEAD_SIZE)
                q = qr[rs, cols]
                do = dor[rs, cols]
                lse = jnp.where(c == 0, lr[rs, h:h + 1], lr[rs, RATIO + h:RATIO + h + 1])
                delta = jnp.sum(do.astype(F32) * orf[rs, cols].astype(F32), axis=1, keepdims=True)
                qa[h, dst, 0:HEAD_SIZE] = q
                qa[h, dst, HEAD_SIZE:] = three(lse * (-1.0 / SCALE), therm)
                doa[h, dst, 0:HEAD_SIZE] = do
                doa[h, dst, HEAD_SIZE:] = three(-delta, zero)
                tdst = pl.ds(pl.multiple_of(h * chip + core * rows + b * blk, blk), blk)
                qt[:, tdst] = q.astype(F32).T.astype(BF)
                dot_[:, tdst] = do.astype(F32).T.astype(BF)

    prepare(q_ref, do_ref, o_ref, lse_ref, mine, c)
    dqacc[...] = jnp.zeros_like(dqacc)
    lane_v = lax.broadcasted_iota(jnp.int32, (chip, HEAD_SIZE), 1)
    ones_tail = jnp.where(lane_v < 3, 1.0, 0.0).astype(BF)

    for r in range(1, nm):
        for w in range(2):
            s0_copy(r, w).wait_recv()

    def ax_copy(d):
        return rcopy(kv.at[x, y], kv.at[x, y], axs.at[d], axr.at[d], (dev(x + d, y, c), z))

    def ay_copy(d, e):
        xs = (x - d + 4) % 4
        return rcopy(kv.at[xs, y], kv.at[xs, y], ays.at[d, e], ayr.at[d, e], (dev(x, y + e, c), z))

    def relay_k(d):
        xs, ys = (x - d + 4) % 4, (y + 3) % 4
        return rcopy(kv.at[xs, ys, 0], kv.at[xs, ys, 0], rks.at[d], rkr.at[d], (dev(x, y + 1, c), z))

    def relay_v(d):
        xs, ys = (x - d + 4) % 4, (y + 1) % 4
        return rcopy(kv.at[xs, ys, 1], kv.at[xs, ys, 1], rvs.at[d], rvr.at[d], (dev(x, y + 3, c), z))

    def ax_wait(d):
        xs = (x - d + 4) % 4
        rcopy(kv.at[xs, y], kv.at[xs, y], axs.at[d], axr.at[d], (dev(x + d, y, c), z)).wait_recv()

    def ay_wait(d, e):
        xs, ys = (x - d + 4) % 4, (y - e + 4) % 4
        rcopy(kv.at[xs, ys], kv.at[xs, ys], ays.at[d, e], ayr.at[d, e], (dev(x, y + e, c), z)).wait_recv()

    def far_wait(d):
        xs, ys = (x - d + 4) % 4, (y + 2) % 4
        rcopy(kv.at[xs, ys, 0], kv.at[xs, ys, 0], rks.at[d], rkr.at[d], (dev(x, y + 1, c), z)).wait_recv()
        rcopy(kv.at[xs, ys, 1], kv.at[xs, ys, 1], rvs.at[d], rvr.at[d], (dev(x, y + 3, c), z)).wait_recv()

    for d in (1, 3, 2):
        ax_copy(d).start()
    for e in (1, 3):
        ay_copy(0, e).start()

    for cp in sib_copies:
        cp.wait_recv()
    prepare(sq, sdo, so, slse, 0, 1 - c)

    def compute(d, e, masked):
        xs, ys = (x - d + 4) % 4, (y - e + 4) % 4
        kb = (xs * 4 + ys) * 4
        for b in range(4):
            ktail[b * blk:(b + 1) * blk, :] = jnp.broadcast_to(
                ktab_ref[pl.ds(kb + b, 1), :], (blk, HEAD_SIZE)).astype(BF)
        key = kv[xs, ys, 0]
        ka = jnp.concatenate([key, ktail[...]], axis=1)
        va = jnp.concatenate([kv[xs, ys, 1], ones_tail], axis=1)
        nt = (((1,), (1,)), ((), ()))
        for h in range(RATIO):
            sc = lax.dot_general(qa[h], ka, nt, preferred_element_type=F32)
            dp = lax.dot_general(doa[h], va, nt, preferred_element_type=F32)
            p = jnp.exp2(sc * (SCALE * LOG2E))
            if masked:
                row = lax.broadcasted_iota(jnp.int32, p.shape, 0)
                col = lax.broadcasted_iota(jnp.int32, p.shape, 1)
                p = jnp.where((col > row) & (col // blk == row // blk), 0.0, p)
            ds = (p * dp).astype(BF)
            pbig[h * chip:(h + 1) * chip, :] = p.astype(BF)
            dsbig[h * chip:(h + 1) * chip, :] = ds
            dqacc[h] += jnp.dot(ds, key, preferred_element_type=F32)
        pbuf[d, e, 0] = (jnp.dot(qt[...], dsbig[...], preferred_element_type=F32) * SCALE).astype(BF)
        pbuf[d, e, 1] = jnp.dot(dot_[...], pbig[...], preferred_element_type=F32).astype(BF)

    def r1_copy(d, e):
        return rcopy(pbuf.at[d, e], r1.at[d, e], r1s.at[d, e], r1r.at[d, e], (dev(x - d + 4, y, c), z))

    def r2_copy(e):
        return rcopy(s2.at[e], r2.at[e], r2s.at[e], r2r.at[e], (dev(x, y - e + 4, c), z))

    def sum_x(e, w):
        tot = pbuf[0, e, w].astype(F32)
        for d in (1, 2, 3):
            tot = tot + r1[d, e, w].astype(F32)
        return tot

    def combine(e):
        for d in (1, 2, 3):
            r1_copy(d, e).wait_recv()
        for w in range(2):
            s2[e, w] = sum_x(e, w).astype(BF)

    compute(0, 0, True)

    def step(t, carry):
        d, e = chunk_of(t)

        @pl.when(e == 0)
        def _():
            ax_wait(d)
            ay_copy(d, 1).start()
            ay_copy(d, 3).start()

        @pl.when(e == 1)
        def _():
            ay_wait(d, 1)
            relay_k(d).start()

        @pl.when(e == 3)
        def _():
            ay_wait(d, 3)
            relay_v(d).start()

        @pl.when(e == 2)
        def _():
            far_wait(d)

        pd, pe = chunk_of(t - 1)

        @pl.when(pd != 0)
        def _():
            r1_copy(pd, pe).start()

        @pl.when(t == 15)
        def _():
            r2_copy(1).start()

        compute(d, e, False)

        @pl.when(t == 14)
        def _():
            combine(1)

        @pl.when(t == 15)
        def _():
            combine(3)

        return carry

    lax.fori_loop(1, 16, step, 0)
    r1_copy(2, 2).start()
    r2_copy(3).start()

    orow = pl.multiple_of((1 - c) * rows, rows)
    mrow = pl.multiple_of(c * rows, rows)
    for h in range(RATIO):
        dqs[:, h * HEAD_SIZE:(h + 1) * HEAD_SIZE] = (dqacc[h, pl.ds(orow, rows), :] * SCALE).astype(BF)
    for h in range(RATIO):
        cols = pl.ds(pl.multiple_of(mine + h * HEAD_SIZE, HEAD_SIZE), HEAD_SIZE)
        dq_ref[:, cols] = (dqacc[h, pl.ds(mrow, rows), :] * SCALE).astype(BF)
    dq_copy = rcopy(dqs, dq_ref.at[:, pl.ds(mine, half)], dqss.at[0], dqsr.at[0], sib)
    dq_copy.start()

    combine(2)
    for d in (1, 2, 3):
        r1_copy(d, 0).wait_recv()
    tots = [sum_x(0, w) for w in range(2)]
    r2_copy(2).start()
    for e in (1, 3):
        r2_copy(e).wait_recv()
        tots = [tots[w] + r2[e, w].astype(F32) for w in range(2)]
    r2_copy(2).wait_recv()
    for w in range(2):
        fin[w] = (tots[w] + r2[2, w].astype(F32)).T.astype(BF)

    def s4_copy(r, w):
        cc, zz = member(r)
        off = pl.multiple_of(cc * rows + zz * piece, piece)
        dst = (dk_ref, dv_ref)[w].at[:, pl.ds(own_g, HEAD_SIZE)]
        return rcopy(fin.at[w, pl.ds(off, piece), :], dst, s4s.at[r, w], s4r.at[r, w], (dev(x, y, cc), zz))

    for r in range(1, nm):
        for w in range(2):
            s4_copy(r, w).start()
    dk_ref[:, pl.ds(own_g, HEAD_SIZE)] = fin[0, pl.ds(own_off, piece), :]
    dv_ref[:, pl.ds(own_g, HEAD_SIZE)] = fin[1, pl.ds(own_off, piece), :]

    def s4_wait(r, w):
        m = (me - r + nm) % nm
        cc, zz = m // nz, m % nz
        g = pl.multiple_of((2 * zz + cc) * HEAD_SIZE, HEAD_SIZE)
        dst = (dk_ref, dv_ref)[w].at[:, pl.ds(g, HEAD_SIZE)]
        rcopy(fin.at[w, pl.ds(0, piece), :], dst, s4s.at[r, w], s4r.at[r, w], sib).wait_recv()

    for r in range(1, nm):
        for w in range(2):
            s4_wait(r, w)
    rcopy(dqs, dq_ref.at[:, pl.ds(other, half)], dqss.at[0], dqsr.at[0], sib).wait_recv()

    for r in range(1, nm):
        for w in range(2):
            s0_copy(r, w).wait_send()
            s4_copy(r, w).wait_send()
    for cp in sib_copies:
        cp.wait_send()
    dq_copy.wait_send()
    for d in (1, 2, 3):
        ax_copy(d).wait_send()
    for e in (1, 2, 3):
        r2_copy(e).wait_send()
    for d in range(4):
        ay_copy(d, 1).wait_send()
        ay_copy(d, 3).wait_send()
        relay_k(d).wait_send()
        relay_v(d).wait_send()
        if d:
            for e in range(4):
                r1_copy(d, e).wait_send()


def fused(nz, queries, keys, values, outputs, out_grad, lse, ktab, qtab):
    rows, piece = queries.shape[0], keys.shape[0]
    chip = 2 * rows
    half = RATIO * HEAD_SIZE
    nm = 2 * nz
    dma = pltpu.SemaphoreType.DMA
    vm = pl.BlockSpec(memory_space=pltpu.VMEM)
    return pl.pallas_call(
        functools.partial(kernel, nz),
        out_shape=(
            jax.ShapeDtypeStruct(queries.shape, BF),
            jax.ShapeDtypeStruct(keys.shape, BF),
            jax.ShapeDtypeStruct(values.shape, BF),
        ),
        in_specs=[vm] * 8,
        out_specs=(vm, vm, vm),
        scratch_shapes=[
            pltpu.VMEM((4, 4, 2, chip, HEAD_SIZE), BF),
            pltpu.VMEM((rows, half), BF),
            pltpu.VMEM((rows, half), BF),
            pltpu.VMEM((rows, half), BF),
            pltpu.VMEM(lse.shape, F32),
            pltpu.VMEM((RATIO, chip, 2 * HEAD_SIZE), BF),
            pltpu.VMEM((RATIO, chip, 2 * HEAD_SIZE), BF),
            pltpu.VMEM((HEAD_SIZE, RATIO * chip), BF),
            pltpu.VMEM((HEAD_SIZE, RATIO * chip), BF),
            pltpu.VMEM((chip, HEAD_SIZE), BF),
            pltpu.VMEM((RATIO * chip, chip), BF),
            pltpu.VMEM((RATIO * chip, chip), BF),
            pltpu.VMEM((RATIO, chip, HEAD_SIZE), F32),
            pltpu.VMEM((4, 4, 2, HEAD_SIZE, chip), BF),
            pltpu.VMEM((4, 4, 2, HEAD_SIZE, chip), BF),
            pltpu.VMEM((4, 2, HEAD_SIZE, chip), BF),
            pltpu.VMEM((4, 2, HEAD_SIZE, chip), BF),
            pltpu.VMEM((2, chip, HEAD_SIZE), BF),
            pltpu.VMEM((rows, half), BF),
            dma((nm, 2)), dma((nm, 2)), dma((4,)), dma((4,)),
            dma((4,)), dma((4,)), dma((4, 4)), dma((4, 4)),
            dma((4,)), dma((4,)), dma((4,)), dma((4,)),
            dma((4, 4)), dma((4, 4)), dma((4,)), dma((4,)),
            dma((nm, 2)), dma((nm, 2)), dma((1,)), dma((1,)),
        ],
        compiler_params=pltpu.CompilerParams(
            collective_id=0, has_side_effects=True, vmem_limit_bytes=60 * 1024 * 1024),
    )(queries, keys, values, outputs, out_grad, lse, ktab, qtab)


def local(nz, queries, keys, values, outputs, out_grad, log_norm, block_order):
    blocks = block_order.shape[0]
    lane = jnp.arange(HEAD_SIZE, dtype=jnp.int32)[None, :]
    slot = lane - (HEAD_SIZE - blocks)
    pos = block_order[:, None]
    ktab = jnp.where((lane < 3) | (slot == pos), 1.0, 0.0).astype(F32)
    qtab = jnp.where(slot > pos, -BIG, 0.0).astype(F32)
    return fused(nz, queries, keys, values, outputs, out_grad, log_norm.T, ktab, qtab)


def solution(mesh):
    in_specs = (
        P("seq", "head"),
        P(("seq", "head"), None),
        P(("seq", "head"), None),
        P("seq", "head"),
        P("seq", "head"),
        P("head", "seq"),
        P(),
    )
    out_specs = (P("seq", "head"), P(("seq", "head"), None), P(("seq", "head"), None))
    return jax.shard_map(
        functools.partial(local, mesh.shape["head"]), mesh=mesh,
        in_specs=in_specs, out_specs=out_specs, check_vma=False)
```

time: 433 us -> 99.2 us (0.23)
  waiting for transfers between devices: 188 us -> 0 us
  Pallas kernels: 0 us -> 92.6 us
  local copies, waits for them, and re-layouts: 93.6 us -> 4.95 us
  matrix products: 78.1 us -> 0 us
  blocking collectives: 26.7 us -> 0 us
  starting transfers between devices: 17.8 us -> 0 us
  between operations: 15.4 us -> 0.67 us
  loops' own time: 5.91 us -> 0 us
  other arithmetic: 5.56 us -> 0.71 us
    reduce_scatter x1 -> x0, waiting for transfers between devices: 95.9 us -> none  [local(): lax.psum_scatter(grad_q_all.astype(jnp.bfloat16), 'seq', scatter_dimensio...]
    pallas_call x0 -> x1, Pallas kernels: none -> 92.6 us  [fused(): pl.pallas_call(functools.partial(kernel, nz), out_shape=(jax.ShapeDtypeSt...]
    all_gather x1 -> x0, waiting for transfers between devices: 79.5 us -> none  [side_by_side(): lax.all_gather(both, axis, axis=dim, tiled=True)]
    dot_general x40 -> x0, matrix products: 78.1 us -> none  [the longest x8 33.9 us: masked_terms(): jnp.einsum('tgrd,ngd->grtn', dout_blk, v_blk, preferred_element_type=jnp....]
    dynamic_slice x17 -> x0, local copies, waits for them, and re-layouts: 26.8 us -> none  [the longest x8 21.4 us: one(): lax.dynamic_slice_in_dim(dout_piece, i * step, step, 0)]
    all_gather x1 -> x0, blocking collectives: 26.7 us -> none  [side_by_side(): lax.all_gather(both, axis, axis=dim, tiled=True)]
    convert_element_type x5 -> x0, local copies, waits for them, and re-layouts: 23.3 us -> none  [the longest x1 21.6 us: local(): grad_q_all.astype(jnp.bfloat16)]
    split x2 -> x0, local copies, waits for them, and re-layouts: 23 us -> none  [side_by_side(): jnp.split(lax.all_gather(both, axis, axis=dim, tiled=True), ends, axis=al...]
  transfers between devices with their start and end apart: 6 -> 0, of which waited for: 5 -> 0; matrix products, arithmetic and copies ran while one was open for 2% -> 0% of each run, Pallas kernels for 0% -> 0%
where the time goes in v1:
time: 99.2 us; the launch traced here: 98.9 us
  Pallas kernels  92.6 us (93%)
  local copies, waits for them, and re-layouts  4.95 us (5%)
    pallas_call x1, Pallas kernels, fused(): pl.pallas_call(functools.partial(kernel, nz), out_shape=(jax.ShapeDtypeSt...  92.6 us
    unnamed x12, local copies, waits for them, and re-layouts  4.95 us

profile of v1, /device:TPU:1, one launch (start us, length us, event | category | flops | bytes accessed | tf_op | source)
XLA Modules:
  0.0 98.9 jit_solution(1584351222650815517)
XLA Ops:
  0.6 0.0 copy-start.3
  0.7 0.6 copy-done.3
  1.3 0.0 copy-start.2
  1.3 0.7 compare_select_fusion
  2.0 0.0 copy-done.2
  2.0 0.8 copy.10
  2.8 92.6 %shard_map.94 = (bf16[256,1024]{1,0:T(8,128)(2,1)}, bf16[64,1024]{1,0:T(8,128)(2,1)}, bf16[64,1024]{1,0:T(8,128)(2,1)}) custom-call(bf16[256,1024]{1,0:T(8,128)(2,1)} %q_ref.1, bf16[64,1024]{1,0:T(8,128)(2,1)} %k_ref.1, bf16[64,1024]{1,0:T(8,128)(2,1)} %v_ref.1, bf16[256,1024]{1,0:T(8,128)(2,1)} %o_ref.1, bf16[256,1024]{1,0:T(8,128)(2,1)} %do_ref.1, ...), custom_call_target="tpu_custom_call" | custom-call | tf_op jit(solution)/shard_map/pallas_call | solution.py:346
  95.4 0.0 copy-start.1
  95.4 1.9 %copy.14 = bf16[256,1024]{1,0:T(8,128)(2,1)} copy(bf16[256,1024]{1,0:T(8,128)(2,1)} %get-tuple-element.8) | data formatting | bytes 1048576
  97.3 0.0 copy-done.1
  97.3 0.0 copy-start
  97.3 0.7 copy.15
  98.0 0.3 copy-done
  98.3 0.7 copy.16
  (2 shorter events, 0.0 us)
Async XLA Ops:
  0.6 0.7 copy-start.3
  1.3 0.7 copy-start.2
  95.4 1.9 %copy-start.1 = (bf16[64,1024]{1,0:T(8,128)(2,1)S(1)}, bf16[64,1024]{1,0:T(8,128)(2,1)}, u32[]{:S(2)}) copy-start(bf16[64,1024]{1,0:T(8,128)(2,1)} %get-tuple-element.9) | copy-start | bytes 393220
  97.3 1.0 copy-start

commit v2 on v1

v2 whole, which is shorter than its diff:
```python
import functools

import jax
import jax.numpy as jnp
from jax import lax
from jax.experimental import pallas as pl
from jax.experimental.pallas import tpu as pltpu
from jax.sharding import PartitionSpec as P

HEAD_SIZE = 128
RATIO = 4
SCALE = HEAD_SIZE ** (-0.5)
LOG2E = 1.4426950408889634
BIG = 131072.0
MESH = pl.DeviceIdType.MESH
BF = jnp.bfloat16
F32 = jnp.float32


ORDER = (
    (0, 0), (0, 1), (0, 3), (2, 0), (1, 1), (3, 3), (2, 1), (2, 3),
    (3, 1), (1, 3), (2, 2), (0, 2), (1, 2), (3, 2), (1, 0), (3, 0),
)


def pick(t, values):
    out = values[0]
    for i, v in enumerate(values):
        out = jnp.where(t == i, v, out)
    return out


def kernel(
    nz,
    qh, kh, vh, oh, doh, lseh, boh,
    dq_ref, dk_ref, dv_ref,
    q_ref, k_ref, v_ref, o_ref, do_ref, lse_ref, bo_ref,
    kv, sq, sdo, so, slse, lpad, lt, qa, doa, qt, dot_, ktail, pbig, dsbig, dqacc,
    pbuf, r1, ra, s2, r2, fin, dqs,
    ins, s0s, s0r, sbs, sbr, axs, axr, ays, ayr, fxs, fxr, fys, fyr,
    r1s, r1r, ras, rar, r2s, r2r, s4s, s4r, dqss, dqsr,
):
    s = lax.axis_index("seq")
    z = lax.axis_index("head")
    x, y, c = s // 8, (s // 2) % 4, s % 2
    rows = q_ref.shape[0]
    piece = k_ref.shape[0]
    chip = 2 * rows
    blk = rows // 2
    half = RATIO * HEAD_SIZE
    nm = 2 * nz

    def dev(xx, yy, cc):
        return ((xx % 4) * 4 + (yy % 4)) * 2 + cc

    me = c * nz + z

    def member(r):
        m = (me + r) % nm
        return m // nz, m % nz

    loads = [
        pltpu.make_async_copy(src, dst, ins.at[i])
        for i, (src, dst) in enumerate((
            (kh, k_ref), (vh, v_ref), (qh, q_ref), (doh, do_ref), (oh, o_ref), (lseh, lse_ref), (boh, bo_ref)))
    ]
    for cp in loads:
        cp.start()

    barrier = pltpu.get_barrier_semaphore()
    for r in range(1, nm):
        cc, zz = member(r)
        pl.semaphore_signal(barrier, inc=1, device_id=(dev(x, y, cc), zz), device_id_type=MESH)
    for d in (1, 3):
        pl.semaphore_signal(barrier, inc=1, device_id=(dev(x + d, y, c), z), device_id_type=MESH)
    for d in (1, 2, 3):
        pl.semaphore_signal(barrier, inc=1, device_id=(dev(x, y + d, c), z), device_id_type=MESH)
    for cp in loads:
        cp.wait()
    with jax.named_scope('bar'):
        pl.semaphore_wait(barrier, nm - 1 + 5)

    def rcopy(src, dst, ss, rs, to):
        return pltpu.make_async_remote_copy(
            src_ref=src, dst_ref=dst, send_sem=ss, recv_sem=rs,
            device_id=to, device_id_type=MESH)

    def s0_copy(r, w):
        cc, zz = member(r)
        g = pl.multiple_of((2 * zz + cc) * HEAD_SIZE, HEAD_SIZE)
        src = (k_ref, v_ref)[w].at[:, pl.ds(g, HEAD_SIZE)]
        off = pl.multiple_of(c * rows + z * piece, piece)
        return rcopy(src, kv.at[x, y, w, pl.ds(off, piece), :],
                     s0s.at[r, w], s0r.at[r, w], (dev(x, y, cc), zz))

    for r in range(1, nm):
        for w in range(2):
            s0_copy(r, w).start()

    other = pl.multiple_of((1 - c) * half, half)
    mine = pl.multiple_of(c * half, half)
    sib = (dev(x, y, 1 - c), z)
    sib_copies = [
        rcopy(lse_ref, slse, sbs.at[3], sbr.at[3], sib),
        rcopy(q_ref.at[:, pl.ds(other, half)], sq, sbs.at[0], sbr.at[0], sib),
        rcopy(do_ref.at[:, pl.ds(other, half)], sdo, sbs.at[1], sbr.at[1], sib),
        rcopy(o_ref.at[:, pl.ds(other, half)], so, sbs.at[2], sbr.at[2], sib),
    ]
    for cp in sib_copies:
        cp.start()

    own_off = pl.multiple_of(c * rows + z * piece, piece)
    own_g = pl.multiple_of((2 * z + c) * HEAD_SIZE, HEAD_SIZE)
    kv[x, y, 0, pl.ds(own_off, piece), :] = k_ref[:, pl.ds(own_g, HEAD_SIZE)]
    kv[x, y, 1, pl.ds(own_off, piece), :] = v_ref[:, pl.ds(own_g, HEAD_SIZE)]

    lane = lax.broadcasted_iota(jnp.int32, (blk, HEAD_SIZE), 1)
    slot = lane - (HEAD_SIZE - bo_ref.shape[0])

    def three(col, rest):
        hi = col.astype(BF).astype(F32)
        mid = (col - hi).astype(BF).astype(F32)
        lo = col - hi - mid
        return jnp.where(lane == 0, hi, jnp.where(lane == 1, mid, jnp.where(lane == 2, lo, rest))).astype(BF)

    chip_block = (x * 4 + y) * 4
    zero = jnp.zeros((blk, HEAD_SIZE), F32)
    lpad[...] = jnp.zeros_like(lpad)

    def prepare(qr, dor, orf, lr, col0, core):
        lpad[0:2 * RATIO, :] = lr[...]
        lt[...] = lpad[...].T
        for b in range(2):
            rs = pl.ds(b * blk, blk)
            dst = pl.ds(pl.multiple_of(core * rows + b * blk, blk), blk)
            therm = jnp.where(slot > bo_ref[chip_block + 2 * core + b], -BIG, zero)
            for h in range(RATIO):
                cols = pl.ds(pl.multiple_of(col0 + h * HEAD_SIZE, HEAD_SIZE), HEAD_SIZE)
                q = qr[rs, cols]
                do = dor[rs, cols]
                lse = jnp.where(c == 0, lt[rs, h:h + 1], lt[rs, RATIO + h:RATIO + h + 1])
                delta = jnp.sum(do.astype(F32) * orf[rs, cols].astype(F32), axis=1, keepdims=True)
                qa[h, dst, 0:HEAD_SIZE] = q
                qa[h, dst, HEAD_SIZE:] = three(lse * (-1.0 / SCALE), therm)
                doa[h, dst, 0:HEAD_SIZE] = do
                doa[h, dst, HEAD_SIZE:] = three(-delta, zero)
                tdst = pl.ds(pl.multiple_of(h * chip + core * rows + b * blk, blk), blk)
                qt[:, tdst] = q.astype(F32).T.astype(BF)
                dot_[:, tdst] = do.astype(F32).T.astype(BF)

    with jax.named_scope('prep0'):
        prepare(q_ref, do_ref, o_ref, lse_ref, mine, c)
    dqacc[...] = jnp.zeros_like(dqacc)
    lane_v = lax.broadcasted_iota(jnp.int32, (chip, HEAD_SIZE), 1)
    ones_tail = jnp.where(lane_v < 3, 1.0, 0.0).astype(BF)
    with jax.named_scope('sibwait'):
        for cp in sib_copies:
            cp.wait_recv()
    with jax.named_scope('prep1'):
        prepare(sq, sdo, so, slse, 0, 1 - c)

    with jax.named_scope('s0wait'):
        for r in range(1, nm):
            for w in range(2):
                s0_copy(r, w).wait_recv()

    def at(d, e):
        return kv.at[(x - d + 4) % 4, (y - e + 4) % 4]

    xp, xm = (dev(x + 1, y, c), z), (dev(x + 3, y, c), z)
    yp, ym = (dev(x, y + 1, c), z), (dev(x, y + 3, c), z)

    def ax(d, chunk):
        return rcopy(chunk, chunk, axs.at[d], axr.at[d], xp if d == 1 else xm)

    def fx(w, chunk):
        return rcopy(chunk.at[w], chunk.at[w], fxs.at[w], fxr.at[w], (xp, xm)[w])

    def ay(d, e, chunk):
        return rcopy(chunk, chunk, ays.at[d, e], ayr.at[d, e], yp if e == 1 else ym)

    def fy(d, w, chunk):
        return rcopy(chunk.at[w], chunk.at[w], fys.at[d, w], fyr.at[d, w], (yp, ym)[w])

    ax(1, at(0, 0)).start()
    ax(3, at(0, 0)).start()
    ay(0, 1, at(0, 0)).start()
    ay(0, 3, at(0, 0)).start()

    def compute(d, e, masked):
        xs, ys = (x - d + 4) % 4, (y - e + 4) % 4
        kb = (xs * 4 + ys) * 4
        for b in range(4):
            ktail[b * blk:(b + 1) * blk, :] = jnp.where(
                (lane < 3) | (slot == bo_ref[kb + b]), 1.0, zero).astype(BF)
        key = kv[xs, ys, 0]
        ka = jnp.concatenate([key, ktail[...]], axis=1)
        va = jnp.concatenate([kv[xs, ys, 1], ones_tail], axis=1)
        nt = (((1,), (1,)), ((), ()))
        for h in range(RATIO):
            sc = lax.dot_general(qa[h], ka, nt, preferred_element_type=F32)
            dp = lax.dot_general(doa[h], va, nt, preferred_element_type=F32)
            p = jnp.exp2(sc * (SCALE * LOG2E))
            if masked:
                row = lax.broadcasted_iota(jnp.int32, p.shape, 0)
                col = lax.broadcasted_iota(jnp.int32, p.shape, 1)
                p = jnp.where((col > row) & (col // blk == row // blk), 0.0, p)
            ds = (p * dp).astype(BF)
            pbig[h * chip:(h + 1) * chip, :] = p.astype(BF)
            dsbig[h * chip:(h + 1) * chip, :] = ds
            dqacc[h] += jnp.dot(ds, key, preferred_element_type=F32)
        pbuf[d, e, 0] = (jnp.dot(qt[...], dsbig[...], preferred_element_type=F32) * SCALE).astype(BF)
        pbuf[d, e, 1] = jnp.dot(dot_[...], pbig[...], preferred_element_type=F32).astype(BF)

    def relay(e, w):
        return rcopy(pbuf.at[2, e, w], ra.at[e, w], ras.at[e, w], rar.at[e, w], (xm, xp)[w])

    def near(d, e, w):
        i = (d - 1) // 2
        return rcopy(pbuf.at[d, e, w], r1.at[i, e, w], r1s.at[i, e, w], r1r.at[i, e, w], xm if d == 1 else xp)

    def r2_copy(e, w):
        return rcopy(s2.at[e, w], r2.at[e, w], r2s.at[e, w], r2r.at[e, w], (dev(x, y - e + 4, c), z))

    def relays(e):
        relay(e, 0).start()
        relay(e, 1).start()

    def plain(d, e):
        near(d, e, 1 if d == 1 else 0).start()

    def join(d, e):
        w = 0 if d == 1 else 1
        with jax.named_scope('ra'):
            relay(e, w).wait_recv()
        pbuf[d, e, w] = (pbuf[d, e, w].astype(F32) + ra[e, w].astype(F32)).astype(BF)
        near(d, e, w).start()

    def sum_x(e, w):
        with jax.named_scope('r1'):
            near(1, e, w).wait_recv()
            near(3, e, w).wait_recv()
        return pbuf[0, e, w].astype(F32) + r1[0, e, w].astype(F32) + r1[1, e, w].astype(F32)

    def combine(e):
        for w in range(2):
            s2[e, w] = sum_x(e, w).astype(BF)

    def got_x():
        ax(1, at(1, 0)).wait_recv()
        ay(1, 1, at(1, 0)).start()
        fx(0, at(1, 0)).start()
        ax(3, at(3, 0)).wait_recv()
        ay(3, 3, at(3, 0)).start()
        fx(1, at(3, 0)).start()
        ay(0, 1, at(0, 1)).wait_recv()

    def got_far_x():
        fx(0, at(2, 0)).wait_recv()
        fx(1, at(2, 0)).wait_recv()
        ay(2, 1, at(2, 0)).start()
        ay(2, 3, at(2, 0)).start()
        ay(3, 1, at(3, 0)).start()
        ay(1, 3, at(1, 0)).start()

    def got_y(d, e):
        ay(d, e, at(d, e)).wait_recv()

    def far_k(d):
        fy(d, 0, at(d, 1)).start()

    def far_v(d):
        fy(d, 1, at(d, 3)).start()

    def got_far_y(d):
        fy(d, 0, at(d, 2)).wait_recv()
        fy(d, 1, at(d, 2)).wait_recv()

    def r2_send(e):
        r2_copy(e, 0).start()
        r2_copy(e, 1).start()

    events = {
        1: lambda: got_x(),
        2: lambda: got_y(0, 3),
        3: lambda: got_far_x(),
        4: lambda: (got_y(1, 1), relays(0)),
        5: lambda: (got_y(3, 3), plain(1, 1)),
        6: lambda: (got_y(2, 1), far_k(2), plain(3, 3)),
        7: lambda: (got_y(2, 3), far_v(2), relays(1)),
        8: lambda: (got_y(3, 1), far_k(0), far_v(0), relays(3)),
        9: lambda: (got_y(1, 3), plain(3, 1), far_k(1), far_v(1), far_k(3), far_v(3)),
        10: lambda: (got_far_y(2), plain(1, 3), join(1, 1), join(3, 1)),
        11: lambda: (got_far_y(0), relays(2), join(3, 3), join(1, 3)),
        12: lambda: got_far_y(1),
        13: lambda: (got_far_y(3), combine(1)),
        14: lambda: (plain(3, 2), join(1, 2), plain(1, 2), join(3, 2), r2_send(1), combine(3)),
        15: lambda: (plain(1, 0), join(1, 0), r2_send(3)),
    }

    with jax.named_scope('comp0'):
        compute(0, 0, True)

    def step(t, carry):
        for g in range(4):
            @pl.when(t // 4 == g)
            def _():
                for k in range(max(1, 4 * g), 4 * g + 4):
                    @pl.when(t == k)
                    def _():
                        with jax.named_scope('ev%d' % k):
                            events[k]()
        with jax.named_scope('comp'):
            compute(pick(t, [o[0] for o in ORDER]), pick(t, [o[1] for o in ORDER]), False)
        return carry

    lax.fori_loop(1, 16, step, 0)
    plain(3, 0)
    join(3, 0)

    orow = pl.multiple_of((1 - c) * rows, rows)
    mrow = pl.multiple_of(c * rows, rows)
    with jax.named_scope('dq'):
        for h in range(RATIO):
            dqs[:, h * HEAD_SIZE:(h + 1) * HEAD_SIZE] = (dqacc[h, pl.ds(orow, rows), :] * SCALE).astype(BF)
        for h in range(RATIO):
            cols = pl.ds(pl.multiple_of(mine + h * HEAD_SIZE, HEAD_SIZE), HEAD_SIZE)
            dq_ref[:, cols] = (dqacc[h, pl.ds(mrow, rows), :] * SCALE).astype(BF)
    for w in range(2):
        s2[2, w] = sum_x(2, w).astype(BF)
        r2_copy(2, w).start()
    dq_copy = rcopy(dqs, dq_ref.at[:, pl.ds(mine, half)], dqss.at[0], dqsr.at[0], sib)
    dq_copy.start()

    def s4_copy(r, w):
        cc, zz = member(r)
        off = pl.multiple_of(cc * rows + zz * piece, piece)
        dst = (dk_ref, dv_ref)[w].at[:, pl.ds(own_g, HEAD_SIZE)]
        return rcopy(fin.at[w, pl.ds(off, piece), :], dst, s4s.at[r, w], s4r.at[r, w], (dev(x, y, cc), zz))

    for w in range(2):
        tot = sum_x(0, w)
        for e in (1, 3, 2):
            with jax.named_scope('r2w'):
                r2_copy(e, w).wait_recv()
            tot = tot + r2[e, w].astype(F32)
        fin[w] = tot.T.astype(BF)
        for r in range(1, nm):
            s4_copy(r, w).start()
    dk_ref[:, pl.ds(own_g, HEAD_SIZE)] = fin[0, pl.ds(own_off, piece), :]
    dv_ref[:, pl.ds(own_g, HEAD_SIZE)] = fin[1, pl.ds(own_off, piece), :]

    def s4_wait(r, w):
        m = (me - r + nm) % nm
        cc, zz = m // nz, m % nz
        g = pl.multiple_of((2 * zz + cc) * HEAD_SIZE, HEAD_SIZE)
        dst = (dk_ref, dv_ref)[w].at[:, pl.ds(g, HEAD_SIZE)]
        rcopy(fin.at[w, pl.ds(0, piece), :], dst, s4s.at[r, w], s4r.at[r, w], sib).wait_recv()

    with jax.named_scope('s4w'):
        for r in range(1, nm):
            for w in range(2):
                s4_wait(r, w)
    rcopy(dqs, dq_ref.at[:, pl.ds(other, half)], dqss.at[0], dqsr.at[0], sib).wait_recv()

    for r in range(1, nm):
        for w in range(2):
            s0_copy(r, w).wait_send()
            s4_copy(r, w).wait_send()
    for cp in sib_copies:
        cp.wait_send()
    dq_copy.wait_send()
    for d in (1, 3):
        ax(d, at(0, 0)).wait_send()
    for w in range(2):
        fx(w, at(0, 0)).wait_send()
        for e in (1, 2, 3):
            r2_copy(e, w).wait_send()
        for e in range(4):
            relay(e, w).wait_send()
            near(1, e, w).wait_send()
            near(3, e, w).wait_send()
        for d in range(4):
            fy(d, w, at(0, 0)).wait_send()
    for d in range(4):
        ay(d, 1, at(0, 0)).wait_send()
        ay(d, 3, at(0, 0)).wait_send()


def fused(nz, queries, keys, values, outputs, out_grad, log_norm, block_order):
    rows, piece = queries.shape[0], keys.shape[0]
    chip = 2 * rows
    half = RATIO * HEAD_SIZE
    nm = 2 * nz
    dma = pltpu.SemaphoreType.DMA
    vm = pl.BlockSpec(memory_space=pltpu.VMEM)
    hbm = pl.BlockSpec(memory_space=pltpu.HBM)
    return pl.pallas_call(
        functools.partial(kernel, nz),
        out_shape=(
            jax.ShapeDtypeStruct(queries.shape, BF),
            jax.ShapeDtypeStruct(keys.shape, BF),
            jax.ShapeDtypeStruct(values.shape, BF),
        ),
        in_specs=[hbm] * 7,
        out_specs=(vm, vm, vm),
        scratch_shapes=[
            pltpu.VMEM(queries.shape, BF),
            pltpu.VMEM(keys.shape, BF),
            pltpu.VMEM(values.shape, BF),
            pltpu.VMEM(outputs.shape, BF),
            pltpu.VMEM(out_grad.shape, BF),
            pltpu.VMEM(log_norm.shape, F32),
            pltpu.SMEM(block_order.shape, jnp.int32),
            pltpu.VMEM((4, 4, 2, chip, HEAD_SIZE), BF),
            pltpu.VMEM((rows, half), BF),
            pltpu.VMEM((rows, half), BF),
            pltpu.VMEM((rows, half), BF),
            pltpu.VMEM(log_norm.shape, F32),
            pltpu.VMEM((HEAD_SIZE, rows), F32),
            pltpu.VMEM((rows, HEAD_SIZE), F32),
            pltpu.VMEM((RATIO, chip, 2 * HEAD_SIZE), BF),
            pltpu.VMEM((RATIO, chip, 2 * HEAD_SIZE), BF),
            pltpu.VMEM((HEAD_SIZE, RATIO * chip), BF),
            pltpu.VMEM((HEAD_SIZE, RATIO * chip), BF),
            pltpu.VMEM((chip, HEAD_SIZE), BF),
            pltpu.VMEM((RATIO * chip, chip), BF),
            pltpu.VMEM((RATIO * chip, chip), BF),
            pltpu.VMEM((RATIO, chip, HEAD_SIZE), F32),
            pltpu.VMEM((4, 4, 2, HEAD_SIZE, chip), BF),
            pltpu.VMEM((2, 4, 2, HEAD_SIZE, chip), BF),
            pltpu.VMEM((4, 2, HEAD_SIZE, chip), BF),
            pltpu.VMEM((4, 2, HEAD_SIZE, chip), BF),
            pltpu.VMEM((4, 2, HEAD_SIZE, chip), BF),
            pltpu.VMEM((2, chip, HEAD_SIZE), BF),
            pltpu.VMEM((rows, half), BF),
            dma((7,)),
            dma((nm, 2)), dma((nm, 2)), dma((4,)), dma((4,)),
            dma((4,)), dma((4,)), dma((4, 4)), dma((4, 4)),
            dma((2,)), dma((2,)), dma((4, 2)), dma((4, 2)),
            dma((2, 4, 2)), dma((2, 4, 2)), dma((4, 2)), dma((4, 2)),
            dma((4, 2)), dma((4, 2)), dma((nm, 2)), dma((nm, 2)), dma((1,)), dma((1,)),
        ],
        compiler_params=pltpu.CompilerParams(
            collective_id=0, has_side_effects=True, vmem_limit_bytes=40 * 1024 * 1024),
    )(*(pltpu.with_memory_space_constraint(a, pltpu.HBM) for a in (
        queries, keys, values, outputs, out_grad, log_norm, block_order)))


def solution(mesh):
    in_specs = (
        P("seq", "head"),
        P(("seq", "head"), None),
        P(("seq", "head"), None),
        P("seq", "head"),
        P("seq", "head"),
        P("head", "seq"),
        P(),
    )
    out_specs = (P("seq", "head"), P(("seq", "head"), None), P(("seq", "head"), None))
    return jax.shard_map(
        functools.partial(fused, mesh.shape["head"]), mesh=mesh,
        in_specs=in_specs, out_specs=out_specs, check_vma=False)
```

time: 99.2 us -> 79.7 us (0.80)
  Pallas kernels: 92.6 us -> 76.8 us
  local copies, waits for them, and re-layouts: 4.95 us -> 2.11 us
    pallas_call x1, Pallas kernels: 92.6 us -> 76.8 us  [fused(): pl.pallas_call(functools.partial(kernel, nz), out_shape=(jax.ShapeDtypeSt...]
    unnamed x12 -> x3, local copies, waits for them, and re-layouts: 4.95 us -> 2.11 us
where the time goes in v2:
time: 79.7 us; the launch traced here: 79.5 us
  Pallas kernels  76.8 us (96%)
  local copies, waits for them, and re-layouts  2.11 us (3%)
    pallas_call x1, Pallas kernels, fused(): pl.pallas_call(functools.partial(kernel, nz), out_shape=(jax.ShapeDtypeSt...  76.8 us
    unnamed x3, local copies, waits for them, and re-layouts  2.11 us

profile of v2, /device:TPU:1, one launch (start us, length us, event | category | flops | bytes accessed | tf_op | source)
XLA Modules:
  0.0 79.5 jit_solution(17375846581979549636)
XLA Ops:
  0.6 76.8 %shard_map.94 = (bf16[256,1024]{1,0:T(8,128)(2,1)S(1)}, bf16[64,1024]{1,0:T(8,128)(2,1)S(1)}, bf16[64,1024]{1,0:T(8,128)(2,1)S(1)}) custom-call(bf16[256,1024]{1,0:T(8,128)(2,1)} %qh.1, bf16[64,1024]{1,0:T(8,128)(2,1)} %kh.1, bf16[64,1024]{1,0:T(8,128)(2,1)} %vh.1, bf16[256,1024]{1,0:T(8,128)(2,1)} %oh.1, bf16[256,1024]{1,0:T(8,128)(2,1)} %doh.1, ...), custom_call_target="tpu_custom_call" | custom-call | tf_op jit(solution)/shard_map/pallas_call | solution.py:398
  77.4 0.8 %copy.13 = bf16[256,1024]{1,0:T(8,128)(2,1)} copy(bf16[256,1024]{1,0:T(8,128)(2,1)S(1)} %get-tuple-element.6) | data formatting | bytes 1048576
  78.2 0.7 copy.14
  78.9 0.7 copy.15

commit v3 on v2

--- a/solution.py
+++ b/solution.py
@@ -53,6 +53,11 @@
     def dev(xx, yy, cc):
         return ((xx % 4) * 4 + (yy % 4)) * 2 + cc
 
+    way = 1 - 2 * c
+
+    def up(p, n):
+        return (p + way * n + 4) % 4
+
     me = c * nz + z
 
     def member(r):
@@ -64,17 +69,16 @@
         for i, (src, dst) in enumerate((
             (kh, k_ref), (vh, v_ref), (qh, q_ref), (doh, do_ref), (oh, o_ref), (lseh, lse_ref), (boh, bo_ref)))
     ]
-    for cp in loads:
-        cp.start()
-
     barrier = pltpu.get_barrier_semaphore()
     for r in range(1, nm):
         cc, zz = member(r)
         pl.semaphore_signal(barrier, inc=1, device_id=(dev(x, y, cc), zz), device_id_type=MESH)
     for d in (1, 3):
-        pl.semaphore_signal(barrier, inc=1, device_id=(dev(x + d, y, c), z), device_id_type=MESH)
+        pl.semaphore_signal(barrier, inc=1, device_id=(dev(up(x, d), y, c), z), device_id_type=MESH)
     for d in (1, 2, 3):
-        pl.semaphore_signal(barrier, inc=1, device_id=(dev(x, y + d, c), z), device_id_type=MESH)
+        pl.semaphore_signal(barrier, inc=1, device_id=(dev(x, up(y, d), c), z), device_id_type=MESH)
+    for cp in loads:
+        cp.start()
     for cp in loads:
         cp.wait()
     with jax.named_scope('bar'):
@@ -153,42 +157,42 @@
     dqacc[...] = jnp.zeros_like(dqacc)
     lane_v = lax.broadcasted_iota(jnp.int32, (chip, HEAD_SIZE), 1)
     ones_tail = jnp.where(lane_v < 3, 1.0, 0.0).astype(BF)
+    with jax.named_scope('s0wait'):
+        for r in range(1, nm):
+            for w in range(2):
+                s0_copy(r, w).wait_recv()
+
+    def at(d, e):
+        return kv.at[up(x, -d), up(y, -e)]
+
+    xp, xm = (dev(up(x, 1), y, c), z), (dev(up(x, -1), y, c), z)
+    yp, ym = (dev(x, up(y, 1), c), z), (dev(x, up(y, -1), c), z)
+
+    def ax(d, chunk):
+        return rcopy(chunk, chunk, axs.at[d], axr.at[d], xp if d == 1 else xm)
+
+    def fx(w, chunk):
+        return rcopy(chunk.at[w], chunk.at[w], fxs.at[w], fxr.at[w], (xp, xm)[w])
+
+    def ay(d, e, chunk):
+        return rcopy(chunk, chunk, ays.at[d, e], ayr.at[d, e], yp if e == 1 else ym)
+
+    def fy(d, w, chunk):
+        return rcopy(chunk.at[w], chunk.at[w], fys.at[d, w], fyr.at[d, w], (yp, ym)[w])
+
+    ax(1, at(0, 0)).start()
+    ax(3, at(0, 0)).start()
+    ay(0, 1, at(0, 0)).start()
+    ay(0, 3, at(0, 0)).start()
+
     with jax.named_scope('sibwait'):
         for cp in sib_copies:
             cp.wait_recv()
     with jax.named_scope('prep1'):
         prepare(sq, sdo, so, slse, 0, 1 - c)
 
-    with jax.named_scope('s0wait'):
-        for r in range(1, nm):
-            for w in range(2):
-                s0_copy(r, w).wait_recv()
-
-    def at(d, e):
-        return kv.at[(x - d + 4) % 4, (y - e + 4) % 4]
-
-    xp, xm = (dev(x + 1, y, c), z), (dev(x + 3, y, c), z)
-    yp, ym = (dev(x, y + 1, c), z), (dev(x, y + 3, c), z)
-
-    def ax(d, chunk):
-        return rcopy(chunk, chunk, axs.at[d], axr.at[d], xp if d == 1 else xm)
-
-    def fx(w, chunk):
-        return rcopy(chunk.at[w], chunk.at[w], fxs.at[w], fxr.at[w], (xp, xm)[w])
-
-    def ay(d, e, chunk):
-        return rcopy(chunk, chunk, ays.at[d, e], ayr.at[d, e], yp if e == 1 else ym)
-
-    def fy(d, w, chunk):
-        return rcopy(chunk.at[w], chunk.at[w], fys.at[d, w], fyr.at[d, w], (yp, ym)[w])
-
-    ax(1, at(0, 0)).start()
-    ax(3, at(0, 0)).start()
-    ay(0, 1, at(0, 0)).start()
-    ay(0, 3, at(0, 0)).start()
-
     def compute(d, e, masked):
-        xs, ys = (x - d + 4) % 4, (y - e + 4) % 4
+        xs, ys = up(x, -d), up(y, -e)
         kb = (xs * 4 + ys) * 4
         for b in range(4):
             ktail[b * blk:(b + 1) * blk, :] = jnp.where(
@@ -220,7 +224,7 @@
         return rcopy(pbuf.at[d, e, w], r1.at[i, e, w], r1s.at[i, e, w], r1r.at[i, e, w], xm if d == 1 else xp)
 
     def r2_copy(e, w):
-        return rcopy(s2.at[e, w], r2.at[e, w], r2s.at[e, w], r2r.at[e, w], (dev(x, y - e + 4, c), z))
+        return rcopy(s2.at[e, w], r2.at[e, w], r2s.at[e, w], r2r.at[e, w], (dev(x, up(y, -e), c), z))
 
     def relays(e):
         relay(e, 0).start()

time: 79.7 us -> 78.5 us (0.985)
  Pallas kernels: 76.8 us -> 75.6 us
    pallas_call x1, Pallas kernels: 76.8 us -> 75.6 us  [fused(): pl.pallas_call(functools.partial(kernel, nz), out_shape=(jax.ShapeDtypeSt...]
where the time goes in v3:
time: 78.5 us; the launch traced here: 78.3 us
  Pallas kernels  75.6 us (96%)
  local copies, waits for them, and re-layouts  2.11 us (3%)
    pallas_call x1, Pallas kernels, fused(): pl.pallas_call(functools.partial(kernel, nz), out_shape=(jax.ShapeDtypeSt...  75.6 us
    unnamed x3, local copies, waits for them, and re-layouts  2.11 us

profile of v3, /device:TPU:1, one launch (start us, length us, event | category | flops | bytes accessed | tf_op | source)
XLA Modules:
  0.0 78.3 jit_solution(12120195312244261823)
XLA Ops:
  0.6 75.6 %shard_map.94 = (bf16[256,1024]{1,0:T(8,128)(2,1)S(1)}, bf16[64,1024]{1,0:T(8,128)(2,1)S(1)}, bf16[64,1024]{1,0:T(8,128)(2,1)S(1)}) custom-call(bf16[256,1024]{1,0:T(8,128)(2,1)} %qh.1, bf16[64,1024]{1,0:T(8,128)(2,1)} %kh.1, bf16[64,1024]{1,0:T(8,128)(2,1)} %vh.1, bf16[256,1024]{1,0:T(8,128)(2,1)} %oh.1, bf16[256,1024]{1,0:T(8,128)(2,1)} %doh.1, ...), custom_call_target="tpu_custom_call" | custom-call | tf_op jit(solution)/shard_map/pallas_call | solution.py:402
  76.2 0.8 %copy.13 = bf16[256,1024]{1,0:T(8,128)(2,1)} copy(bf16[256,1024]{1,0:T(8,128)(2,1)S(1)} %get-tuple-element.6) | data formatting | bytes 1048576
  77.0 0.7 copy.14
  77.7 0.7 copy.15

commit v4 on v3

--- a/solution.py
+++ b/solution.py
@@ -212,7 +212,8 @@
             ds = (p * dp).astype(BF)
             pbig[h * chip:(h + 1) * chip, :] = p.astype(BF)
             dsbig[h * chip:(h + 1) * chip, :] = ds
-            dqacc[h] += jnp.dot(ds, key, preferred_element_type=F32)
+        for h in range(RATIO):
+            dqacc[h] += jnp.dot(dsbig[h * chip:(h + 1) * chip, :], key, preferred_element_type=F32)
         pbuf[d, e, 0] = (jnp.dot(qt[...], dsbig[...], preferred_element_type=F32) * SCALE).astype(BF)
         pbuf[d, e, 1] = jnp.dot(dot_[...], pbig[...], preferred_element_type=F32).astype(BF)
 
@@ -315,7 +316,8 @@
                         with jax.named_scope('ev%d' % k):
                             events[k]()
         with jax.named_scope('comp'):
-            compute(pick(t, [o[0] for o in ORDER]), pick(t, [o[1] for o in ORDER]), False)
+            code = pick(t, [d + 4 * e for d, e in ORDER])
+            compute(lax.rem(code, 4), lax.div(code, 4), False)
         return carry
 
     lax.fori_loop(1, 16, step, 0)

time: 78.5 us -> 78.5 us (level)
  no operation moved by 1% of the time
where the time goes in v4:
time: 78.5 us; the launch traced here: 78.4 us
  Pallas kernels  75.6 us (96%)
  local copies, waits for them, and re-layouts  2.11 us (3%)
    pallas_call x1, Pallas kernels, fused(): pl.pallas_call(functools.partial(kernel, nz), out_shape=(jax.ShapeDtypeSt...  75.6 us
    unnamed x3, local copies, waits for them, and re-layouts  2.11 us

profile of v4, /device:TPU:1, one launch (start us, length us, event | category | flops | bytes accessed | tf_op | source)
XLA Modules:
  0.0 78.4 jit_solution(11902526616765110983)
XLA Ops:
  0.6 75.6 %shard_map.94 = (bf16[256,1024]{1,0:T(8,128)(2,1)S(1)}, bf16[64,1024]{1,0:T(8,128)(2,1)S(1)}, bf16[64,1024]{1,0:T(8,128)(2,1)S(1)}) custom-call(bf16[256,1024]{1,0:T(8,128)(2,1)} %qh.1, bf16[64,1024]{1,0:T(8,128)(2,1)} %kh.1, bf16[64,1024]{1,0:T(8,128)(2,1)} %vh.1, bf16[256,1024]{1,0:T(8,128)(2,1)} %oh.1, bf16[256,1024]{1,0:T(8,128)(2,1)} %doh.1, ...), custom_call_target="tpu_custom_call" | custom-call | tf_op jit(solution)/shard_map/pallas_call | solution.py:404
  76.3 0.8 %copy.13 = bf16[256,1024]{1,0:T(8,128)(2,1)} copy(bf16[256,1024]{1,0:T(8,128)(2,1)S(1)} %get-tuple-element.6) | data formatting | bytes 1048576
  77.1 0.7 copy.14
  77.7 0.7 copy.15
